TPU v7x, 128 devices: a whole 4x4x4 slice. The times are simulated.
128 devices in a mesh: dp: 128 (over z, y, x, core).
Axes of the slice: x: 4, y: 4, z: 4, core: 2. Of those that a mesh axis runs over, the one named last changes fastest.
Arguments:
- attended: bfloat16 [65536, 1152], P('dp'), may hold values from -24 to 24, as said below
- proj_cot: bfloat16 [65536, 1152], P('dp'), may hold values from -0.00036621094 to 0.00036621094
- timesteps: float32 [256], P('dp'), may hold values from 0 to 1
- embed_cot: bfloat16 [256, 1152], P('dp'), may hold values from -0.015625 to 0.015625
- master_proj: float32 [1327104], P('dp'), may hold values from -0.1875 to 0.1875
- moment_proj: float32 [1327104], P('dp'), may hold values from -0.013671875 to 0.013671875
- second_proj: float32 [1327104], P('dp'), may hold values from 1.8838011e-07 to 3.0140818e-06
- master_embed: float32 [294912], P('dp'), may hold values from -0.375 to 0.375
- moment_embed: float32 [294912], P('dp'), may hold values from -0.02734375 to 0.02734375
- squared_moment_layer: float32 [294912], P('dp'), may hold values from 8.477105e-07 to 1.3563368e-05
- attended_next: bfloat16 [65536, 1152], P('dp'), may hold values from -6 to 6
- timesteps_next: float32 [256], P('dp'), may hold values from 0 to 1
Outputs:
- next_proj: bfloat16 [65536, 1152], P('dp')
- next_embed: bfloat16 [256, 1152], P('dp')
- move_direction_output: float32 [1327104], P('dp')
- step_embed: float32 [294912], P('dp')
- master_proj_new: float32 [1327104], P('dp')
- master_embed_new: float32 [294912], P('dp')
- grad_norm: float32 [], replicated
Inputs may be any that keep to these rules, and one draw needn't show every extreme that they name: attended has entries of mean zero whose scale differs between feature columns by up to a factor of 16.
All inputs are finite; a program needn't handle non-finite values.
Results may differ from a plain program's by a relative error of at most 0.0025.
Values may be sent and summed in bfloat16 or wider, within the bound.
A program may use at most 64 MiB of HBM per device.

v0:
```python
import math
import jax
import jax.numpy as jnp
from jax import lax
from jax.sharding import Mesh
from jax.sharding import PartitionSpec as P

DP = ("dp_0", "dp_1", "dp_2", "dp_3")
beta_one = 0.9
beta_two = 0.999
step_count = 1000.0
learn_rate = 0.0001
shrink_factor = 0.01
epsilon = 1e-08
max_norm = 1.0


def over_axes(value, axes):
    for axis in axes:
        value = lax.psum(value, axis)
    return value


def joined_along(blocks, dim):
    lengths = list(blocks.shape[1:])
    lengths[dim] *= blocks.shape[0]
    return jnp.moveaxis(blocks, 0, dim).reshape(lengths)


def gather_packed(arrays, axis, dims):
    flat = jnp.concatenate([a.reshape(-1) for a in arrays])
    lines, at, finished = (lax.all_gather(flat, axis), 0, [])
    for a, dim in zip(arrays, dims):
        blocks = lines[:, at : at + a.size].reshape(-1, *a.shape)
        finished.append(joined_along(blocks, dim))
        at += a.size
    return tuple(finished)


def freq_embed(moments, width):
    half_width = width // 2
    ladder = jnp.arange(half_width, dtype=jnp.float32)
    freqs = jnp.exp(-math.log(10000.0) * ladder / half_width)
    phase_values = (moments * 1000.0)[:, None] * freqs[None, :]
    return jnp.concatenate([jnp.cos(phase_values), jnp.sin(phase_values)], axis=1).astype(
        jnp.bfloat16
    )


def adamw_update(gradient, clip, master, moment, second):
    scaled = clip * gradient
    first_new = beta_one * moment + (1.0 - beta_one) * scaled
    second_new = beta_two * second + (1.0 - beta_two) * scaled * scaled
    first_hat = first_new / (1.0 - beta_one**step_count)
    second_hat = second_new / (1.0 - beta_two**step_count)
    direction = first_hat / (jnp.sqrt(second_hat) + epsilon)
    freshened_values = master - learn_rate * (direction + shrink_factor * master)
    return (direction, freshened_values)


def shards(
    attended,
    proj_cot,
    timesteps,
    embed_cot,
    master_proj,
    moment_proj,
    second_proj,
    master_embed,
    moment_embed,
    squared_moment_layer,
    attended_next,
    timesteps_next,
):
    width = attended.shape[1]
    freq_width = master_embed.shape[0] * lax.axis_size(DP) // width
    term_proj = jnp.dot(attended.T, proj_cot, preferred_element_type=jnp.float32).reshape(-1)
    freq_now = freq_embed(timesteps, freq_width)
    term_embed = jnp.dot(freq_now.T, embed_cot, preferred_element_type=jnp.float32).reshape(-1)
    grad_proj, grad_embed = (
        lax.psum_scatter(term_proj, DP, scatter_dimension=0, tiled=True),
        lax.psum_scatter(term_embed, DP, scatter_dimension=0, tiled=True),
    )
    square_proj = over_axes(jnp.sum(grad_proj * grad_proj), DP)
    square_embed = over_axes(jnp.sum(grad_embed * grad_embed), DP)
    total = square_proj + square_embed
    grad_norm = jnp.sqrt(total)
    clip = jnp.minimum(jnp.float32(1.0), max_norm / (grad_norm + 1e-06))
    move_direction_output, master_proj_new = adamw_update(
        grad_proj, clip, master_proj, moment_proj, second_proj
    )
    step_embed, master_embed_new = adamw_update(
        grad_embed, clip, master_embed, moment_embed, squared_moment_layer
    )
    shard_proj = master_proj_new.astype(jnp.bfloat16)
    shard_embed = master_embed_new.astype(jnp.bfloat16)
    whole_proj, whole_embed = gather_packed((shard_proj, shard_embed), DP, (0, 0))
    weight_proj = whole_proj.reshape(width, width)
    weight_embed = whole_embed.reshape(freq_width, width)
    next_proj = jnp.dot(attended_next, weight_proj, preferred_element_type=jnp.float32).astype(
        jnp.bfloat16
    )
    freq_next = freq_embed(timesteps_next, freq_width)
    next_embed = jnp.dot(freq_next, weight_embed, preferred_element_type=jnp.float32).astype(
        jnp.bfloat16
    )
    return (
        next_proj,
        next_embed,
        move_direction_output,
        step_embed,
        master_proj_new,
        master_embed_new,
        grad_norm,
    )


def solution(mesh):
    finer = Mesh(mesh.devices.reshape(4, 4, 4, 2), ("dp_0", "dp_1", "dp_2", "dp_3"))
    return jax.shard_map(
        shards,
        mesh=finer,
        in_specs=(
            P(DP, None),
            P(DP, None),
            P(DP),
            P(DP, None),
            P(DP),
            P(DP),
            P(DP),
            P(DP),
            P(DP),
            P(DP),
            P(DP, None),
            P(DP),
        ),
        out_specs=(P(DP, None), P(DP, None), P(DP), P(DP), P(DP), P(DP), P()),
        check_vma=False,
    )
```

profile of v0, /device:TPU:1, one launch (start us, length us, event | category | flops | bytes accessed | tf_op | source)
XLA Modules:
  0.0 314.4 jit_solution(12199632284855341670)
XLA Ops:
  7.2 0.0 copy-start
  7.2 0.0 all-reduce.5.cloned.1.call-start
  7.2 0.8 broadcast_multiply_fusion
  8.0 0.1 fusion.13
  8.1 1.1 fusion.15
  9.2 0.0 copy-start.1
  9.2 1.1 reshape.28
  10.3 0.0 copy-done
  10.3 0.6 copy-done.1
  10.9 4.1 %fusion.28 = f32[1152,1152]{1,0:T(8,128)} fusion(bf16[512,1152]{1,0:T(8,128)(2,1)S(1)} %copy-done, bf16[512,1152]{1,0:T(8,128)(2,1)S(1)} %copy-done.1), kind=kOutput, calls=%fused_computation.43 | convolution fusion | flops 1358954496 | bytes 7667712 | tf_op jit(solution)/shard_map/dot_general | solution.py:77
  15.0 6.6 %reshape.27 = f32[1327104]{0:T(1024)} reshape(f32[1152,1152]{1,0:T(8,128)} %fusion.28) | data formatting | bytes 10616832 | tf_op jit(solution)/shard_map/reshape | solution.py:77
  21.5 0.0 copy-start.2
  21.5 0.0 copy-start.3
  21.5 0.0 copy-start.4
  21.5 0.0 copy-start.5
  21.5 0.0 copy-start.6
  21.5 0.0 copy-start.7
  21.5 0.0 all-reduce.5.cloned.1.call-update
  21.6 0.0 all-gather.4.cloned.1.call-start
  21.6 161.1 %all-reduce.5.cloned.1.call-done = (f32[294912]{0:T(1024)}, f32[1327104]{0:T(1024)}) async-done(((f32[294912]{0:T(1024)}, f32[1327104]{0:T(1024)}), (f32[294912]{0:T(1024)}, f32[1327104]{0:T(1024)})) %all-reduce.5.cloned.1.call-update) | async-done | bytes 6488080
  182.8 1.5 multiply_reduce_fusion
  184.2 1.4 multiply_reduce_fusion.1
  186.9 9.0 %psum.67 = f32[]{:T(128)} all-reduce(f32[]{:T(128)S(6)} %add.56), channel_id=1, replica_groups=mesh['dp_0'=4,'dp_1'=4,'dp_2'=4,'dp_3'=2] {'dp_0'}, use_global_device_ids=true, to_apply=%region_2.0 | all-reduce | flops 1 | bytes 8 | tf_op jit(solution)/shard_map/psum | solution.py:20
  195.9 7.8 %psum.66 = f32[]{:T(128)} all-reduce(f32[]{:T(128)} %psum.67), channel_id=1, replica_groups=mesh['dp_0'=4,'dp_1'=4,'dp_2'=4,'dp_3'=2] {'dp_1'}, use_global_device_ids=true, to_apply=%region_3.0 | all-reduce | flops 1 | bytes 8 | tf_op jit(solution)/shard_map/psum | solution.py:20
  203.7 7.8 %psum.65 = f32[]{:T(128)} all-reduce(f32[]{:T(128)} %psum.66), channel_id=1, replica_groups=mesh['dp_0'=4,'dp_1'=4,'dp_2'=4,'dp_3'=2] {'dp_2'}, use_global_device_ids=true, to_apply=%region_4.0 | all-reduce | flops 1 | bytes 8 | tf_op jit(solution)/shard_map/psum | solution.py:20
  211.5 9.2 %psum.64 = f32[]{:T(128)} all-reduce(f32[]{:T(128)} %psum.65), channel_id=1, replica_groups=mesh['dp_0'=4,'dp_1'=4,'dp_2'=4,'dp_3'=2] {'dp_3'}, use_global_device_ids=true, to_apply=%region_5.0 | all-reduce | flops 1 | bytes 8 | tf_op jit(solution)/shard_map/psum | solution.py:20
  221.5 0.0 copy-done.2
  221.5 0.0 copy-done.3
  221.5 0.0 copy-done.4
  221.5 1.6 fusion.24
  223.1 0.0 copy-done.5
  223.1 0.0 copy-done.6
  223.1 0.0 copy-done.7
  223.1 1.4 fusion.26
  224.5 0.6 reshape.30
  225.2 0.0 all-gather.4.cloned.1.call-update
  225.2 63.7 %all-gather.4.cloned.1.call-done = bf16[128,1,12672]{2,1,0:T(2,128)(2,1)} async-done(((bf16[1,1,12672]{2,1,0:T(2,128)(2,1)}), bf16[128,1,12672]{2,1,0:T(2,128)(2,1)}) %all-gather.4.cloned.1.call-update) | async-done | bytes 3244048 | tf_op jit(solution)/shard_map/all_gather | solution.py:32
  288.9 3.2 %copy.24 = bf16[128,1,12672]{2,0,1:T(8,128)(2,1)S(1)} copy(bf16[128,1,12672]{2,1,0:T(2,128)(2,1)} %all-gather.4.cloned.1.call-done) | data formatting | bytes 6488064
  292.1 1.7 slice.8
  293.9 6.4 %reshape_reshape.6 = bf16[1152,1152]{1,0:T(8,128)(2,1)} reshape(bf16[128,10368]{1,0:T(8,128)(2,1)} %slice.8) | data formatting | bytes 5308416 | tf_op jit(solution)/shard_map/reshape;reshape | solution.py:98
  300.2 3.8 %fusion = bf16[512,1152]{0,1:T(8,128)(2,1)S(1)} fusion(bf16[1152,1152]{1,0:T(8,128)(2,1)} %reshape_reshape.6, bf16[512,1152]{1,0:T(8,128)(2,1)} %param.22), kind=kOutput, calls=%fused_computation.2 | convolution fusion | flops 1359544320 | bytes 5013504 | tf_op jit(solution)/shard_map/dot_general | solution.py:100
  304.0 1.4 copy.21
  305.5 0.2 reshape_reshape.7
  305.7 0.8 convolution_convert_fusion.1
  (3 shorter events, 0.1 us)
Async XLA Ops:
  7.2 3.1 copy-start
  7.2 175.6 %all-reduce.5.cloned.1.call-start = ((), (), s32[]{:S(2)}) async-start(), calls=%async_computation.1 | async-start | bytes 12976128
  9.2 1.7 copy-start.1
  21.5 200.0 %copy-start.2 = (f32[10368]{0:T(1024)S(1)}, f32[10368]{0:T(1024)}, u32[]{:S(2)}) copy-start(f32[10368]{0:T(1024)} %param.16) | copy-start | bytes 124420
  21.5 200.0 %copy-start.3 = (f32[10368]{0:T(1024)S(1)}, f32[10368]{0:T(1024)}, u32[]{:S(2)}) copy-start(f32[10368]{0:T(1024)} %param.18) | copy-start | bytes 124420
  21.5 200.0 %copy-start.4 = (f32[10368]{0:T(1024)S(1)}, f32[10368]{0:T(1024)}, u32[]{:S(2)}) copy-start(f32[10368]{0:T(1024)} %param.17) | copy-start | bytes 124420
  21.5 201.6 %copy-start.5 = (f32[2304]{0:T(1024)S(1)}, f32[2304]{0:T(1024)}, u32[]{:S(2)}) copy-start(f32[2304]{0:T(1024)} %param.19) | copy-start | bytes 27652
  21.5 201.6 %copy-start.6 = (f32[2304]{0:T(1024)S(1)}, f32[2304]{0:T(1024)}, u32[]{:S(2)}) copy-start(f32[2304]{0:T(1024)} %param.21) | copy-start | bytes 27652
  21.5 201.6 %copy-start.7 = (f32[2304]{0:T(1024)S(1)}, f32[2304]{0:T(1024)}, u32[]{:S(2)}) copy-start(f32[2304]{0:T(1024)} %param.20) | copy-start | bytes 27652
  21.6 267.4 %all-gather.4.cloned.1.call-start = ((), (), s32[]{:S(2)}) async-start(), calls=%async_computation | async-start | bytes 6538752 | tf_op jit(solution)/shard_map/all_gather | solution.py:32
Sparse Core Ops, SparseCore 0:
  21.7 161.0 all-reduce.4
  225.3 63.5 all-gather.3
where the time goes:
time: 315 us; the launch traced here: 314 us
  waiting for transfers between devices  225 us (71%)
  blocking collectives  33.8 us (11%)
  local copies, waits for them, and re-layouts  21.8 us (7%)
  between operations  17.3 us (5%)
  matrix products  9.73 us (3%)
  other arithmetic  6.77 us (2%)
    unnamed x3, waiting for transfers between devices  161 us
    all_gather x1, waiting for transfers between devices, gather_packed(): lines, at, finished = (lax.all_gather(flat, axis), 0, [])  63.7 us
    psum x4, blocking collectives, over_axes(): value = lax.psum(value, axis)  33.8 us
    reshape x1, local copies, waits for them, and re-layouts, shards(): jnp.dot(attended.T, proj_cot, preferred_element_type=jnp.float32)  6.55 us
    another operation x1, local copies, waits for them, and re-layouts, shards(): weight_proj = whole_proj.reshape(width, width)  6.36 us
  transfers between devices with their start and end apart: 2, of which 2 were waited for; matrix products, arithmetic and copies ran while one was open for 0% of the time, Pallas kernels for 0%

commit v1 on v0

--- a/solution.py
+++ b/solution.py
@@ -17,7 +17,7 @@
 
 def over_axes(value, axes):
     for axis in axes:
-        value = lax.psum(value, axis)
+        value = jnp.sum(lax.all_gather(value, axis), axis=0)
     return value
 
 

time: 315 us -> 330 us (1.048)
  local copies, waits for them, and re-layouts: 21.8 us -> 35.9 us
  other arithmetic: 6.77 us -> 11.6 us
    psum x4 -> x0, blocking collectives: 33.8 us -> none  [over_axes(): value = lax.psum(value, axis)]
    unnamed x0 -> x4, blocking collectives: none -> 31.4 us
    unnamed x19 -> x47, local copies, waits for them, and re-layouts: 5.88 us -> 19.9 us
    reduce_sum x0 -> x8, other arithmetic: none -> 4.81 us  [over_axes(): value = jnp.sum(lax.all_gather(value, axis), axis=0)]
where the time goes in v1:
time: 330 us; the launch traced here: 329 us
  waiting for transfers between devices  224 us (68%)
  local copies, waits for them, and re-layouts  35.9 us (11%)
  blocking collectives  31.4 us (10%)
  between operations  16.7 us (5%)
  other arithmetic  11.6 us (4%)
  matrix products  9.73 us (3%)
    unnamed x3, waiting for transfers between devices  160 us
    all_gather x1, waiting for transfers between devices, gather_packed(): lines, at, finished = (lax.all_gather(flat, axis), 0, [])  63.7 us
    unnamed x4, blocking collectives  31.4 us
    unnamed x47, local copies, waits for them, and re-layouts  19.9 us
  transfers between devices with their start and end apart: 2, of which 2 were waited for; matrix products, arithmetic and copies ran while one was open for 0% of the time, Pallas kernels for 0%

profile of v1, /device:TPU:1, one launch (start us, length us, event | category | flops | bytes accessed | tf_op | source)
XLA Modules:
  0.0 329.2 jit_solution(6638782126000948072)
XLA Ops:
  7.2 0.0 copy-start
  7.2 0.0 all-reduce.17.cloned.1.call-start
  7.2 0.8 broadcast_multiply_fusion
  8.0 0.1 fusion.13
  8.1 1.1 fusion.15
  9.2 0.0 copy-start.1
  9.2 1.1 reshape.28
  10.3 0.0 copy-done
  10.3 0.6 copy-done.1
  10.9 4.1 %fusion.28 = f32[1152,1152]{1,0:T(8,128)} fusion(bf16[512,1152]{1,0:T(8,128)(2,1)S(1)} %copy-done, bf16[512,1152]{1,0:T(8,128)(2,1)S(1)} %copy-done.1), kind=kOutput, calls=%fused_computation.43 | convolution fusion | flops 1358954496 | bytes 7667712 | tf_op jit(solution)/shard_map/dot_general | solution.py:77
  15.0 6.6 %reshape.27 = f32[1327104]{0:T(1024)} reshape(f32[1152,1152]{1,0:T(8,128)} %fusion.28) | data formatting | bytes 10616832 | tf_op jit(solution)/shard_map/reshape | solution.py:77
  21.5 0.0 copy-start.2
  21.5 0.0 copy-start.3
  21.5 0.0 copy-start.4
  21.6 0.0 copy-start.5
  21.6 0.0 copy-start.6
  21.6 0.0 copy-start.7
  21.6 0.0 all-reduce.17.cloned.1.call-update
  21.6 0.0 all-gather.4.cloned.1.call-start
  21.7 0.5 copy-done.11
  22.2 0.6 dynamic-slice
  22.7 160.1 %all-reduce.17.cloned.1.call-done = (f32[294912]{0:T(1024)}, f32[1327104]{0:T(1024)}) async-done(((f32[294912]{0:T(1024)}, f32[1327104]{0:T(1024)}), (f32[294912]{0:T(1024)}, f32[1327104]{0:T(1024)})) %all-reduce.17.cloned.1.call-update) | async-done | bytes 6488080
  182.8 1.5 multiply_reduce_fusion
  184.3 1.4 multiply_reduce_fusion.1
  185.7 1.4 dynamic-update-slice
  187.1 1.4 dynamic-update-slice.4
  188.5 0.0 copy-done.10
  188.5 0.6 dynamic-slice.1
  189.1 8.4 %all-reduce.13 = (f32[4]{0:T(128)S(1)}, f32[4]{0:T(128)S(1)}) all-reduce(f32[4]{0:T(128)S(1)} %dynamic-update-slice, f32[4]{0:T(128)S(1)} %dynamic-update-slice.4), channel_id=1, replica_groups=mesh['dp_0'=4,'dp_1'=4,'dp_2'=4,'dp_3'=2] {'dp_0'}, use_global_device_ids=true, to_apply=%add | all-reduce | flops 8 | bytes 64
  197.5 0.6 reduce_sum.96
  198.1 0.6 reduce_sum.91
  198.7 1.4 dynamic-update-slice.5
  200.1 1.4 dynamic-update-slice.1
  201.5 0.6 dynamic-slice.2
  202.1 7.2 %all-reduce.12 = (f32[4]{0:T(128)S(1)}, f32[4]{0:T(128)S(1)}) all-reduce(f32[4]{0:T(128)S(1)} %dynamic-update-slice.1, f32[4]{0:T(128)S(1)} %dynamic-update-slice.5), channel_id=1, replica_groups=mesh['dp_0'=4,'dp_1'=4,'dp_2'=4,'dp_3'=2] {'dp_1'}, use_global_device_ids=true, to_apply=%add.1 | all-reduce | flops 8 | bytes 64
  209.3 0.6 reduce_sum.97
  209.9 0.6 reduce_sum.92
  210.5 1.4 dynamic-update-slice.6
  211.9 1.4 dynamic-update-slice.2
  213.3 0.0 copy-done.8
  213.3 0.6 dynamic-slice.3
  213.9 7.2 %all-reduce.11 = (f32[4]{0:T(128)S(1)}, f32[4]{0:T(128)S(1)}) all-reduce(f32[4]{0:T(128)S(1)} %dynamic-update-slice.2, f32[4]{0:T(128)S(1)} %dynamic-update-slice.6), channel_id=1, replica_groups=mesh['dp_0'=4,'dp_1'=4,'dp_2'=4,'dp_3'=2] {'dp_2'}, use_global_device_ids=true, to_apply=%add.2 | all-reduce | flops 8 | bytes 64
  221.1 0.6 reduce_sum.98
  221.7 0.6 reduce_sum.93
  222.3 1.4 dynamic-update-slice.7
  223.7 1.4 dynamic-update-slice.3
  225.1 8.6 %all-reduce.14 = (f32[2]{0:T(128)S(1)}, f32[2]{0:T(128)S(1)}) all-reduce(f32[2]{0:T(128)S(1)} %dynamic-update-slice.3, f32[2]{0:T(128)S(1)} %dynamic-update-slice.7), channel_id=1, replica_groups=mesh['dp_0'=4,'dp_1'=4,'dp_2'=4,'dp_3'=2] {'dp_3'}, use_global_device_ids=true, to_apply=%add.3 | all-reduce | flops 4 | bytes 32
  233.7 0.6 reduce_sum.94
  234.3 0.6 reduce_sum.99
  236.3 0.0 copy-done.2
  236.3 0.0 copy-done.3
  236.3 0.0 copy-done.4
  236.3 1.6 fusion.24
  237.9 1.4 fusion.26
  239.3 0.6 reshape.54
  239.9 0.0 all-gather.4.cloned.1.call-update
  240.0 63.7 %all-gather.4.cloned.1.call-done = bf16[128,1,12672]{2,1,0:T(2,128)(2,1)} async-done(((bf16[1,1,12672]{2,1,0:T(2,128)(2,1)}), bf16[128,1,12672]{2,1,0:T(2,128)(2,1)}) %all-gather.4.cloned.1.call-update) | async-done | bytes 3244048 | tf_op jit(solution)/shard_map/all_gather | solution.py:32
  303.7 3.2 copy.24
  306.9 1.7 slice.8
  308.6 6.4 %reshape_reshape.6 = bf16[1152,1152]{1,0:T(8,128)(2,1)} reshape(bf16[128,10368]{1,0:T(8,128)(2,1)} %slice.8) | data formatting | bytes 5308416 | tf_op jit(solution)/shard_map/reshape;reshape | solution.py:98
  315.0 3.8 %fusion = bf16[512,1152]{0,1:T(8,128)(2,1)S(1)} fusion(bf16[1152,1152]{1,0:T(8,128)(2,1)} %reshape_reshape.6, bf16[512,1152]{1,0:T(8,128)(2,1)} %param.22), kind=kOutput, calls=%fused_computation.2 | convolution fusion | flops 1359544320 | bytes 5013504 | tf_op jit(solution)/shard_map/dot_general | solution.py:100
  318.8 1.4 copy.21
  320.2 0.2 reshape_reshape.7
  320.4 0.8 convolution_convert_fusion.1
  (19 shorter events, 0.1 us)
Async XLA Ops:
  7.2 3.1 copy-start
  7.2 175.6 %all-reduce.17.cloned.1.call-start = ((), (), s32[]{:S(2)}) async-start(), calls=%async_computation.1 | async-start | bytes 12976128
  9.2 1.7 copy-start.1
  21.5 0.7 copy-start.11
  21.5 167.0 %copy-start.10 = (u32[128]{0:T(128)S(1)}, u32[128]{0:T(128)}, u32[]{:S(2)}) copy-start(u32[128]{0:T(128)} %constant.51) | copy-start | bytes 1540
  21.5 180.0 %copy-start.9 = (u32[128]{0:T(128)S(1)}, u32[128]{0:T(128)}, u32[]{:S(2)}) copy-start(u32[128]{0:T(128)} %constant.56) | copy-start | bytes 1540
  21.5 191.8 %copy-start.8 = (u32[128]{0:T(128)S(1)}, u32[128]{0:T(128)}, u32[]{:S(2)}) copy-start(u32[128]{0:T(128)} %constant.61) | copy-start | bytes 1540
  21.5 214.7 %copy-start.2 = (f32[10368]{0:T(1024)S(1)}, f32[10368]{0:T(1024)}, u32[]{:S(2)}) copy-start(f32[10368]{0:T(1024)} %param.16) | copy-start | bytes 124420
  21.5 214.7 %copy-start.3 = (f32[10368]{0:T(1024)S(1)}, f32[10368]{0:T(1024)}, u32[]{:S(2)}) copy-start(f32[10368]{0:T(1024)} %param.18) | copy-start | bytes 124420
  21.5 214.7 %copy-start.4 = (f32[10368]{0:T(1024)S(1)}, f32[10368]{0:T(1024)}, u32[]{:S(2)}) copy-start(f32[10368]{0:T(1024)} %param.17) | copy-start | bytes 124420
  21.6 216.3 %copy-start.5 = (f32[2304]{0:T(1024)S(1)}, f32[2304]{0:T(1024)}, u32[]{:S(2)}) copy-start(f32[2304]{0:T(1024)} %param.19) | copy-start | bytes 27652
  21.6 216.3 %copy-start.6 = (f32[2304]{0:T(1024)S(1)}, f32[2304]{0:T(1024)}, u32[]{:S(2)}) copy-start(f32[2304]{0:T(1024)} %param.21) | copy-start | bytes 27652
  21.6 216.3 %copy-start.7 = (f32[2304]{0:T(1024)S(1)}, f32[2304]{0:T(1024)}, u32[]{:S(2)}) copy-start(f32[2304]{0:T(1024)} %param.20) | copy-start | bytes 27652
  21.6 282.1 %all-gather.4.cloned.1.call-start = ((), (), s32[]{:S(2)}) async-start(), calls=%async_computation | async-start | bytes 6538752 | tf_op jit(solution)/shard_map/all_gather | solution.py:32
Sparse Core Ops, SparseCore 0:
  21.7 161.0 all-reduce.16
  240.1 63.5 all-gather.3
